TPU v7x, 512 devices: a whole 4x4x16 slice. The times are simulated.
512 devices in a mesh: ens: 64 (over y, z_lo, core), slab: 8 (over x, z_hi).
Axes of the slice: x: 4, y: 4, z: 16 (z_hi: 2, z_lo: 8; z = z_hi * 8 + z_lo), core: 2. Of those that a mesh axis runs over, the one named last changes fastest.
Arguments:
- displacement: float32 [192, 24, 24, 128], P('ens', 'slab'), parts along dimension 0, may hold values from -0.75 to 0.75
- velocity: float32 [192, 24, 24, 128], P('ens', 'slab'), parts along dimension 0, may hold values from -6 to 6
- bond_mask: int32 [512, 24, 24, 128], P('ens', 'slab'), parts along dimension 0, may hold values from 0 to 65535, as said below
- moduli: float32 [16, 2], replicated, may hold values from 16 to 64
- material: int32 [64], P('ens'), parts along dimension 0, may hold values from 0 to 15
Outputs:
- new_displacement: float32 [192, 24, 24, 128], P('ens', 'slab'), parts along dimension 0
- new_velocity: float32 [192, 24, 24, 128], P('ens', 'slab'), parts along dimension 0
- energy: float32 [64], P('ens'), parts along dimension 0
There are 64 independent parts, one for each index of `ens`. A program takes and returns all parts, laid end to end along the dimension named above; an argument that names none is the same for every part. Nothing has to cross between parts.
Inputs may be any that keep to these rules, and one draw needn't show every extreme that they name: `bond_mask`: bit number k mod 16 of word k // 16 is 1 where the bond along offset o_k of the list O is intact and 0 where it is broken; the bond along o_k from a cell p and the bond along -o_k from p + o_k carry the same bit wherever both cells lie in the grid; bits 10 to 15 of word 7 are 0.
All inputs are finite; a program needn't handle non-finite values.
Results may differ from a plain program's by a relative error of at most 0.00002.
Values sent between devices are 32-bit elements; how exact they have to be, the bound alone decides.
A program may use at most 64 MiB of HBM per device.

v0:
```python
import functools
import math

import jax
import jax.numpy as jnp
import numpy as np
from jax import lax
from jax.experimental import pallas as pl
from jax.experimental.pallas import tpu as pltpu
from jax.sharding import PartitionSpec as P

DT = 0.125
MESH = pl.DeviceIdType.MESH
F32 = jnp.float32


def offset_list():
    up = []
    for a in range(-3, 4):
        for b in range(-3, 4):
            for c in range(-3, 4):
                if a * a + b * b + c * c <= 9 and (a, b, c) > (0, 0, 0):
                    up.append((a, b, c))
    return up + [(-a, -b, -c) for a, b, c in up]


OFFSETS = offset_list()
NUMBER = {o: k for k, o in enumerate(OFFSETS)}
SLOT = {o: k for k, o in enumerate(sorted(OFFSETS))}


def classes(a):
    found = {}
    for o in sorted(OFFSETS):
        if o[0] == a:
            found.setdefault(a * a + o[1] * o[1] + o[2] * o[2], []).append(o)
    return sorted(found.items())


def signed(bits):
    bits &= 0xFFFFFFFF
    return bits - (1 << 32) if bits >> 31 else bits


def tables(nx, ny, nz, words):
    in_x = np.zeros((nx, words), np.int64)
    in_y = np.zeros((ny, words), np.int64)
    in_z = np.zeros((nz, words), np.int64)
    plane = np.zeros((4, ny, nz), np.float64)
    y, z = np.arange(ny), np.arange(nz)
    for k, (a, b, c) in enumerate(OFFSETS):
        w, bit = k // 16, 1 << (k % 16)
        for x in range(nx):
            in_x[x, w] |= bit * (0 <= x + a < nx)
        ok_y = (0 <= y + b) & (y + b < ny)
        ok_z = (0 <= z + c) & (z + c < nz)
        in_y[:, w] |= bit * ok_y
        in_z[:, w] |= bit * ok_z
        if a >= 0:
            r2 = a * a + b * b + c * c
            plane[a] += math.exp(-r2 / 9.0) * r2 * (ok_y[:, None] & ok_z[None, :])
    in_yz = in_y.T[:, :, None] & in_z.T[:, None, :]
    return in_x.astype(np.int32), in_yz.astype(np.int32), plane.astype(np.float32)


def kernel(
    sx, nx,
    u_hbm, v_hbm, w_hbm, yz_hbm, plane_hbm, moduli, material, in_x,
    nu_hbm, nv_hbm, en_ref,
    U, S, HY, W, YZ, Q, AL, SA, SB, V, ACC, HM, E1, FA, VEL, OV, OU, EB, EP,
    local, out_sem, us, ur, fs, fr, ts, tr, gs, gr, es, er, ps, pr,
):
    ens = lax.axis_index("ens")
    slab = lax.axis_index("slab")
    nxs = sx // 2
    px = slab // 2
    par = slab % 2
    step = 1 - 2 * par
    partner = (ens, slab + step)
    ahead = (ens, slab + 2 * step)
    has_ahead = jnp.logical_and(px + step >= 0, px + step < nxs)
    has_behind = jnp.logical_and(px - step >= 0, px - step < nxs)
    own_x = U.shape[0] // 3
    ny, nz = U.shape[2:]

    def at_x(d):
        return (ens, 2 * ((px + d) % nxs) + par)

    barrier = pltpu.get_barrier_semaphore()
    pl.semaphore_signal(barrier, inc=1, device_id=partner, device_id_type=MESH)
    for d in range(1, nxs):
        pl.semaphore_signal(barrier, inc=1, device_id=at_x(d), device_id_type=MESH)

    def layer(i):
        return i + par * (own_x - 1 - 2 * i)

    loads = []

    def load(src, dst):
        c = pltpu.make_async_copy(src, dst, local.at[len(loads)])
        c.start()
        loads.append(c)
        return c

    u_loads = [load(u_hbm.at[:, layer(i)], U.at[own_x + i]) for i in range(own_x)]
    w_loads = [load(w_hbm.at[:, layer(i)], W.at[i]) for i in range(own_x)]
    w_loads.append(load(yz_hbm, YZ))
    q_load = load(plane_hbm, Q)
    v_loads = [load(v_hbm.at[:, layer(i)], VEL.at[i]) for i in range(own_x)]

    def remote(src, dst, send, recv, dev):
        return pltpu.make_async_remote_copy(
            src_ref=src, dst_ref=dst, send_sem=send, recv_sem=recv, device_id=dev, device_id_type=MESH
        )

    def to_partner(ref, send, recv, i):
        return remote(ref.at[own_x + i], ref.at[3 * own_x - 1 - i], send.at[i], recv.at[i], partner)

    def to_ahead(ref, send, recv, i):
        return remote(ref.at[3 * own_x - 1 - i], ref.at[own_x - 1 - i], send.at[i], recv.at[i], ahead)

    for c in u_loads:
        c.wait()
    pl.semaphore_wait(barrier, nxs)
    for i in range(own_x):
        to_partner(U, us, ur, i).start()

    sign = step.astype(F32)
    bulk = moduli[material[0], 0]
    shear = moduli[material[0], 1]
    zero = jnp.zeros((8, nz), F32)

    def clear(L, _):
        for c in range(7):
            for comp in range(3):
                S[c, L, comp, 0:8] = zero
                S[c, L, comp, 8 + ny : 16 + ny] = zero
            for ref in (SA, SB):
                ref[c, L, 0:8] = zero
                ref[c, L, 8 + ny : 16 + ny] = zero
        return 0

    lax.fori_loop(0, 3 * own_x, clear, 0)

    @pl.when(jnp.logical_not(has_behind))
    def _():
        for L in range(own_x):
            for comp in range(3):
                U[L, comp] = jnp.zeros((ny, nz), F32)
            AL[L] = jnp.zeros((ny, nz), F32)

    def rolled(x, c):
        return x if c == 0 else pltpu.roll(x, (-c) % nz, 1)

    def shift_u(L, reach):
        ux = U[L, 0] * sign
        uy = U[L, 1]
        uz = U[L, 2]
        for c in range(-reach, reach + 1):
            S[c + 3, L, 0, 8 : 8 + ny] = rolled(ux, c)
            S[c + 3, L, 1, 8 : 8 + ny] = rolled(uy, c)
            S[c + 3, L, 2, 8 : 8 + ny] = rolled(uz, c) + float(c)

    def shift_to(ref, L, x, reach):
        for c in range(-reach, reach + 1):
            ref[c + 3, L, 8 : 8 + ny] = rolled(x, c)

    def prepare(i, _):
        shift_u(own_x + i, 3)
        uy = U[own_x + i, 1]
        for b in range(-3, 4):
            HY[b + 3, i] = uy - float(b)
        for n in range(3):
            ACC[n, i] = jnp.zeros((ny, nz), F32)
            FA[n, i] = jnp.zeros((ny, nz), F32)
        return 0

    lax.fori_loop(0, own_x, prepare, 0)
    for c in w_loads:
        c.wait()
    base = own_x * slab

    def clean(i, _):
        x = base + layer(i)
        for n in range(W.shape[1]):
            W[i, n] = W[i, n] & YZ[n] & in_x[x * W.shape[1] + n]
        return 0

    lax.fori_loop(0, own_x, clean, 0)

    def bond(a, b, c, i, L, hx, hz):
        rows = slice(8 + b, 8 + b + ny)
        bx = S[c + 3, L, 0, rows] - hx
        by = S[c + 3, L, 1, rows] - HY[b + 3, i]
        bz = S[c + 3, L, 2, rows] - hz
        return bx, by, bz

    def first(a, i):
        L = own_x + i + a
        hx = U[own_x + i, 0] * sign - float(a)
        hz = U[own_x + i, 2]
        total = [jnp.zeros((ny, nz), F32)] * 3
        for r2, offs in classes(a):
            r, wt = math.sqrt(r2), math.exp(-r2 / 9.0)
            s1 = s2 = s0 = None
            for _, b, c in offs:
                bx, by, bz = bond(a, b, c, i, L, hx, hz)
                sq = bx * bx + by * by + bz * bz
                inv = lax.rsqrt(sq)
                st = sq * inv - r
                kp, km = NUMBER[(a, b, c)], NUMBER[(-a, b, c)]
                word = kp // 16 + par * (km // 16 - kp // 16)
                bit = (1 << (kp % 16)) + par * ((1 << (km % 16)) - (1 << (kp % 16)))
                live = (W[i, word] & bit) != 0
                ms = jnp.where(live, st, 0.0)
                hm = jnp.where(live, inv, 0.0)
                one = jnp.where(live, 1.0, 0.0)
                HM[SLOT[(a, b, c)], i] = hm * r
                E1[SLOT[(a, b, c)], i] = ms * hm
                s1 = ms if s1 is None else s1 + ms
                s2 = ms * ms if s2 is None else s2 + ms * ms
                s0 = one if s0 is None else s0 + one
            total = [total[0] + (wt * r) * s1, total[1] + wt * s2, total[2] + (wt * r2) * s0]
        for n in range(3):
            ACC[n, i] += total[n]

    def second(a, i):
        L = own_x + i + a
        hx = U[own_x + i, 0] * sign - float(a)
        hz = U[own_x + i, 2]
        ah = AL[own_x + i]
        bh = SB[3, own_x + i, 8 : 8 + ny]
        total = [jnp.zeros((ny, nz), F32)] * 3
        for r2, offs in classes(a):
            wt = math.exp(-r2 / 9.0)
            f = [None] * 3
            for _, b, c in offs:
                rows = slice(8 + b, 8 + b + ny)
                k = SLOT[(a, b, c)]
                t = (bh + SB[c + 3, L, rows]) * E1[k, i] + (ah + SA[c + 3, L, rows]) * HM[k, i]
                y = bond(a, b, c, i, L, hx, hz)
                f = [t * y[n] if f[n] is None else f[n] + t * y[n] for n in range(3)]
            total = [total[n] + wt * f[n] for n in range(3)]
        for n in range(3):
            FA[n, i] += total[n]

    def inner(block):
        def at(a, lo, hi):
            def one(i, _):
                block(a, i)
                return 0

            lax.fori_loop(lo, hi, one, 0)

        for a in range(-2, 3):
            at(a, max(0, -a), own_x - max(0, a))

    def outer(block, L):
        for i in range(own_x):
            a = L - own_x - i
            if -3 <= a <= 3:
                block(a, i)

    inner(first)

    q_load.wait()

    def volumes(L, _):
        x = base + layer(L - own_x)
        sums = jnp.zeros((ny, nz), F32)
        for a in range(4):
            up = jnp.logical_and(x + a >= 0, x + a < nx).astype(F32)
            down = jnp.logical_and(x - a >= 0, x - a < nx).astype(F32)
            sums = sums + (up if a == 0 else up + down) * Q[a]
        home = jnp.logical_and(x >= 0, x < nx)
        vol = jnp.where(home, sums, 1.0)
        V[L] = vol
        shift_to(SB, L, 15.0 * shear / vol, 3)
        return 0

    lax.fori_loop(0, 3 * own_x, volumes, 0)

    for i in range(own_x):
        L = 3 * own_x - 1 - i
        to_partner(U, us, ur, i).wait_recv()

        @pl.when(has_ahead)
        def _():
            to_ahead(U, fs, fr, i).start()

        shift_u(L, 2)
        outer(first, L)
    for i in range(own_x):
        L = own_x - 1 - i

        @pl.when(has_behind)
        def _():
            to_ahead(U, fs, fr, i).wait_recv()

        shift_u(L, 2)
        outer(first, L)

    factor = 3.0 * bulk - 5.0 * shear

    def dilate(i, _):
        vol = V[own_x + i]
        AL[own_x + i] = factor * (3.0 * ACC[0, i] / vol) / vol
        return 0

    lax.fori_loop(0, own_x, dilate, 0)

    def shift_a(i, _):
        shift_to(SA, own_x + i, AL[own_x + i], 3)
        return 0

    lax.fori_loop(0, own_x, shift_a, 0)
    for i in range(own_x):
        to_partner(AL, ts, tr, i).start()

    inner(second)

    for i in range(own_x):
        L = 3 * own_x - 1 - i
        to_partner(AL, ts, tr, i).wait_recv()

        @pl.when(has_ahead)
        def _():
            to_ahead(AL, gs, gr, i).start()

        shift_to(SA, L, AL[L], 2)
        outer(second, L)
    for i in range(own_x):
        L = own_x - 1 - i

        @pl.when(has_behind)
        def _():
            to_ahead(AL, gs, gr, i).wait_recv()

        shift_to(SA, L, AL[L], 2)
        outer(second, L)

    for c in v_loads:
        c.wait()
    heat = jnp.zeros((ny, nz), F32)
    for i in range(own_x):
        kinetic = None
        for n in range(3):
            force = FA[n, i] * sign if n == 0 else FA[n, i]
            nv = VEL[i, n] + DT * force
            OV[i, n] = nv
            OU[i, n] = U[own_x + i, n] + DT * nv
            kinetic = nv * nv if kinetic is None else kinetic + nv * nv
        vol = V[own_x + i]
        th = 3.0 * ACC[0, i] / vol
        th2 = th * th
        strain = ACC[1, i] - (2.0 / 9.0) * th2 * vol + th2 * ACC[2, i] * (1.0 / 9.0)
        heat = heat + 0.5 * kinetic + 0.5 * bulk * th2 + 7.5 * shear * strain / vol
    EB[px] = jnp.sum(heat, axis=0, keepdims=True)

    outs = []
    for i in range(own_x):
        for src, dst in ((OV, nv_hbm), (OU, nu_hbm)):
            c = pltpu.make_async_copy(src.at[i], dst.at[:, layer(i)], out_sem.at[len(outs)])
            c.start()
            outs.append(c)

    rows = [remote(EB.at[px], EB.at[px], es.at[d], er.at[px], at_x(d)) for d in range(1, nxs)]
    for c in rows:
        c.start()
    for d in range(1, nxs):
        q = (px + d) % nxs
        remote(EB.at[q], EB.at[q], es.at[d], er.at[q], at_x(d)).wait_recv()
    group = EB[0]
    for n in range(1, nxs):
        group = group + EB[n]
    EP[0] = group
    last = remote(EP.at[0], EP.at[1], ps, pr, partner)
    last.start()
    for c in outs:
        c.wait()
    for i in range(own_x):
        to_partner(U, us, ur, i).wait_send()
        to_partner(AL, ts, tr, i).wait_send()

        @pl.when(has_ahead)
        def _():
            to_ahead(U, fs, fr, i).wait_send()
            to_ahead(AL, gs, gr, i).wait_send()

    for c in rows:
        c.wait_send()
    last.wait_recv()
    both = EP[0] + EP[1]
    en_ref[...] = jnp.broadcast_to(jnp.sum(both, axis=1, keepdims=True), en_ref.shape) * (1.0 / (nx * ny * nz))
    last.wait_send()


def solution(mesh):
    slabs = mesh.shape["slab"]

    def body(displacement, velocity, bond_mask, moduli, material):
        own_x, ny, nz = displacement.shape[1:]
        words = bond_mask.shape[0]
        nx = own_x * slabs
        in_x, in_yz, plane = tables(nx, ny, nz, words)
        grid = (ny, nz)
        tall = (ny + 16, nz)
        nb = len(OFFSETS)
        vm = pltpu.VMEM
        dma = pltpu.SemaphoreType.DMA
        hbm = pl.BlockSpec(memory_space=pl.ANY)
        smem = pl.BlockSpec(memory_space=pltpu.SMEM)
        full = jax.ShapeDtypeStruct(displacement.shape, F32)
        nu, nv, en = pl.pallas_call(
            functools.partial(kernel, slabs, nx),
            out_shape=(full, full, jax.ShapeDtypeStruct((1, nz), F32)),
            in_specs=[hbm] * 5 + [smem] * 3,
            out_specs=(hbm, hbm, pl.BlockSpec(memory_space=pltpu.VMEM)),
            scratch_shapes=[
                vm((3 * own_x, 3) + grid, F32),
                vm((7, 3 * own_x, 3) + tall, F32),
                vm((7, own_x) + grid, F32),
                vm((own_x, words) + grid, jnp.int32),
                vm((words,) + grid, jnp.int32),
                vm((4,) + grid, F32),
                vm((3 * own_x,) + grid, F32),
                vm((7, 3 * own_x) + tall, F32),
                vm((7, 3 * own_x) + tall, F32),
                vm((3 * own_x,) + grid, F32),
                vm((3, own_x) + grid, F32),
                vm((nb, own_x) + grid, F32),
                vm((nb, own_x) + grid, F32),
                vm((3, own_x) + grid, F32),
                vm((own_x, 3) + grid, F32),
                vm((own_x, 3) + grid, F32),
                vm((own_x, 3) + grid, F32),
                vm((slabs // 2, 1, nz), F32),
                vm((2, 1, nz), F32),
                dma((3 * own_x + 2,)),
                dma((2 * own_x,)),
                dma((own_x,)), dma((own_x,)), dma((own_x,)), dma((own_x,)),
                dma((own_x,)), dma((own_x,)), dma((own_x,)), dma((own_x,)),
                dma((slabs // 2,)), dma((slabs // 2,)),
                dma, dma,
            ],
            compiler_params=pltpu.CompilerParams(collective_id=0, has_side_effects=True),
        )(
            displacement, velocity, bond_mask, jnp.asarray(in_yz), jnp.asarray(plane),
            moduli, material, jnp.asarray(in_x.reshape(-1)),
        )
        return nu, nv, en[0, :1]

    in_specs = (
        P("ens", "slab", None, None),
        P("ens", "slab", None, None),
        P("ens", "slab", None, None),
        P(),
        P("ens"),
    )
    out_specs = (P("ens", "slab", None, None), P("ens", "slab", None, None), P("ens"))
    return jax.shard_map(body, mesh=mesh, in_specs=in_specs, out_specs=out_specs, check_vma=False)
```

profile of v0, /device:TPU:40, one launch (start us, length us, event | category | flops | bytes accessed | tf_op | source)
XLA Modules:
  0.0 57.4 jit_solution(14964319325511723688)
XLA Ops:
  0.6 0.0 copy-start.1
  1.3 0.0 copy-done.1
  1.3 0.7 %copy.11.moduli = f32[16,2]{1,0:T(8,128)} copy(f32[16,2]{0,1:T(2,128)S(1)} %copy-done.1) | data formatting | bytes 256 | tf_op args[3]
  2.0 51.9 %shard_map.103 = (f32[3,3,24,128]{3,2,1,0:T(8,128)}, f32[3,3,24,128]{3,2,1,0:T(8,128)}, f32[1,128]{1,0:T(1,128)}) custom-call(f32[3,3,24,128]{3,2,1,0:T(8,128)} %u_hbm.1, f32[3,3,24,128]{3,2,1,0:T(8,128)} %v_hbm.1, s32[8,3,24,128]{3,2,1,0:T(8,128)} %w_hbm.1, s32[8,24,128]{2,1,0:T(8,128)} %constant.6.clone.yz_hbm, f32[4,24,128]{2,1,0:T(8,128)} %constant.7.clone.plane_hbm, ...), custom_call_target="tpu_custom_call" | custom-call | tf_op jit(solution)/shard_map/pallas_call | solution.py:414
  53.9 0.0 copy-start
  54.0 1.6 %copy.16 = f32[3,3,24,128]{3,2,1,0:T(8,128)} copy(f32[3,3,24,128]{3,2,1,0:T(8,128)} %get-tuple-element.12) | data formatting | bytes 221184
  55.5 0.0 copy-done
  55.5 0.0 copy-start.2
  55.5 0.6 %copy.17 = f32[3,3,24,128]{3,2,1,0:T(8,128)} copy(f32[3,3,24,128]{3,2,1,0:T(8,128)S(1)} %copy-done) | data formatting | bytes 221184
  56.2 0.0 copy-done.2
Async XLA Ops:
  0.6 0.7 %copy-start.1 = (f32[16,2]{0,1:T(2,128)S(1)}, f32[16,2]{0,1:T(2,128)}, u32[]{:S(2)}) copy-start(f32[16,2]{0,1:T(2,128)} %param.11) | copy-start | bytes 388
  53.9 1.6 %copy-start = (f32[3,3,24,128]{3,2,1,0:T(8,128)S(1)}, f32[3,3,24,128]{3,2,1,0:T(8,128)}, u32[]{:S(2)}) copy-start(f32[3,3,24,128]{3,2,1,0:T(8,128)} %get-tuple-element.13) | copy-start | bytes 331780
  55.5 0.6 %copy-start.2 = (f32[1,128]{1,0:T(1,128)S(1)}, f32[1,128]{1,0:T(1,128)}, u32[]{:S(2)}) copy-start(f32[1,128]{1,0:T(1,128)} %get-tuple-element.8) | copy-start | bytes 1540
where the time goes:
time: 57.6 us; the launch traced here: 57.4 us
  Pallas kernels  51.9 us (90%)
  local copies, waits for them, and re-layouts  2.93 us (5%)
  between operations  2.48 us (4%)
    pallas_call x1, Pallas kernels, body(): pl.pallas_call(functools.partial(kernel, slabs, nx), out_shape=(full, ful...  51.9 us
    unnamed x9, local copies, waits for them, and re-layouts  2.93 us

commit v1 on v0

--- a/solution.py
+++ b/solution.py
@@ -37,21 +37,17 @@
     return sorted(found.items())
 
 
-def signed(bits):
-    bits &= 0xFFFFFFFF
-    return bits - (1 << 32) if bits >> 31 else bits
-
-
-def tables(nx, ny, nz, words):
-    in_x = np.zeros((nx, words), np.int64)
+def layer_bits(a, word):
+    return sum(1 << (k % 16) for k, o in enumerate(OFFSETS) if o[0] == a and k // 16 == word)
+
+
+def tables(ny, nz, words):
     in_y = np.zeros((ny, words), np.int64)
     in_z = np.zeros((nz, words), np.int64)
     plane = np.zeros((4, ny, nz), np.float64)
     y, z = np.arange(ny), np.arange(nz)
     for k, (a, b, c) in enumerate(OFFSETS):
         w, bit = k // 16, 1 << (k % 16)
-        for x in range(nx):
-            in_x[x, w] |= bit * (0 <= x + a < nx)
         ok_y = (0 <= y + b) & (y + b < ny)
         ok_z = (0 <= z + c) & (z + c < nz)
         in_y[:, w] |= bit * ok_y
@@ -60,15 +56,15 @@
             r2 = a * a + b * b + c * c
             plane[a] += math.exp(-r2 / 9.0) * r2 * (ok_y[:, None] & ok_z[None, :])
     in_yz = in_y.T[:, :, None] & in_z.T[:, None, :]
-    return in_x.astype(np.int32), in_yz.astype(np.int32), plane.astype(np.float32)
+    return in_yz.astype(np.int32), plane.astype(np.float32)
 
 
 def kernel(
     sx, nx,
-    u_hbm, v_hbm, w_hbm, yz_hbm, plane_hbm, moduli, material, in_x,
-    nu_hbm, nv_hbm, en_ref,
-    U, S, HY, W, YZ, Q, AL, SA, SB, V, ACC, HM, E1, FA, VEL, OV, OU, EB, EP,
-    local, out_sem, us, ur, fs, fr, ts, tr, gs, gr, es, er, ps, pr,
+    u_hbm, v_hbm, w_hbm, yz_hbm, plane_hbm, moduli_hbm, material_hbm,
+    force_hbm, en_ref,
+    U, S, HY, W, WS, YZ, Q, SI, CX, RX, AL, SA, SB, V, ACC, HM, E1, FA, VEL, FO, EB, moduli, material,
+    local, out_sem, us, ur, fs, fr, ts, tr, gs, gr, xs, xr, es, er,
 ):
     ens = lax.axis_index("ens")
     slab = lax.axis_index("slab")
@@ -78,13 +74,17 @@
     step = 1 - 2 * par
     partner = (ens, slab + step)
     ahead = (ens, slab + 2 * step)
+    behind = (ens, slab - 2 * step)
     has_ahead = jnp.logical_and(px + step >= 0, px + step < nxs)
     has_behind = jnp.logical_and(px - step >= 0, px - step < nxs)
     own_x = U.shape[0] // 3
     ny, nz = U.shape[2:]
 
+    def slab_at(d, other):
+        return 2 * ((px + d) % nxs) + (1 - par if other else par)
+
     def at_x(d):
-        return (ens, 2 * ((px + d) % nxs) + par)
+        return (ens, slab_at(d, False))
 
     barrier = pltpu.get_barrier_semaphore()
     pl.semaphore_signal(barrier, inc=1, device_id=partner, device_id_type=MESH)
@@ -105,7 +105,7 @@
     u_loads = [load(u_hbm.at[:, layer(i)], U.at[own_x + i]) for i in range(own_x)]
     w_loads = [load(w_hbm.at[:, layer(i)], W.at[i]) for i in range(own_x)]
     w_loads.append(load(yz_hbm, YZ))
-    q_load = load(plane_hbm, Q)
+    q_loads = [load(plane_hbm, Q), load(moduli_hbm, moduli), load(material_hbm, material)]
     v_loads = [load(v_hbm.at[:, layer(i)], VEL.at[i]) for i in range(own_x)]
 
     def remote(src, dst, send, recv, dev):
@@ -119,6 +119,16 @@
     def to_ahead(ref, send, recv, i):
         return remote(ref.at[3 * own_x - 1 - i], ref.at[own_x - 1 - i], send.at[i], recv.at[i], ahead)
 
+    for L in range(own_x):
+
+        @pl.when(jnp.logical_not(has_behind))
+        def _():
+            RX[L] = jnp.zeros((ny, nz), F32)
+
+        @pl.when(jnp.logical_not(has_ahead))
+        def _():
+            RX[2 * own_x + L] = jnp.zeros((ny, nz), F32)
+
     for c in u_loads:
         c.wait()
     pl.semaphore_wait(barrier, nxs)
@@ -126,8 +136,6 @@
         to_partner(U, us, ur, i).start()
 
     sign = step.astype(F32)
-    bulk = moduli[material[0], 0]
-    shear = moduli[material[0], 1]
     zero = jnp.zeros((8, nz), F32)
 
     def clear(L, _):
@@ -147,7 +155,7 @@
         for L in range(own_x):
             for comp in range(3):
                 U[L, comp] = jnp.zeros((ny, nz), F32)
-            AL[L] = jnp.zeros((ny, nz), F32)
+            SI[L] = jnp.zeros((ny, nz), F32)
 
     def rolled(x, c):
         return x if c == 0 else pltpu.roll(x, (-c) % nz, 1)
@@ -182,8 +190,18 @@
 
     def clean(i, _):
         x = base + layer(i)
+        gone = {a: jnp.logical_or(x + a < 0, x + a >= nx).astype(jnp.int32) for a in range(-3, 4) if a}
         for n in range(W.shape[1]):
-            W[i, n] = W[i, n] & YZ[n] & in_x[x * W.shape[1] + n]
+            keep = 0xFFFF
+            for a, out in gone.items():
+                if layer_bits(a, n):
+                    keep = keep - out * layer_bits(a, n)
+            word = W[i, n] & YZ[n] & keep
+            W[i, n] = word
+            for c in range(-2, 3):
+                WS[c + 2, i, n, 0:8] = jnp.zeros((8, nz), jnp.int32)
+                WS[c + 2, i, n, 8 + ny : 16 + ny] = jnp.zeros((8, nz), jnp.int32)
+                WS[c + 2, i, n, 8 : 8 + ny] = rolled(word, c)
         return 0
 
     lax.fori_loop(0, own_x, clean, 0)
@@ -194,6 +212,35 @@
         by = S[c + 3, L, 1, rows] - HY[b + 3, i]
         bz = S[c + 3, L, 2, rows] - hz
         return bx, by, bz
+
+    def where_bit(a, b, c):
+        kp, km = NUMBER[(a, b, c)], NUMBER[(-a, b, c)]
+        word = kp // 16 + par * (km // 16 - kp // 16)
+        bit = (1 << (kp % 16)) + par * ((1 << (km % 16)) - (1 << (kp % 16)))
+        return word, bit
+
+    def across(a, i):
+        L = own_x + i + a
+        hx = U[L, 0] * sign + float(a)
+        hy = U[L, 1]
+        hz = U[L, 2]
+        total = None
+        for r2, offs in classes(a):
+            r, wt = math.sqrt(r2), math.exp(-r2 / 9.0)
+            s1 = None
+            for _, b, c in offs:
+                rows = slice(8 - b, 8 - b + ny)
+                bx = S[3 - c, own_x + i, 0, rows] - hx
+                by = S[3 - c, own_x + i, 1, rows] - (hy + float(b))
+                bz = S[3 - c, own_x + i, 2, rows] - hz
+                sq = bx * bx + by * by + bz * bz
+                st = sq * lax.rsqrt(sq) - r
+                word, bit = where_bit(a, b, c)
+                live = (WS[2 - c, i, word, rows] & bit) != 0
+                ms = jnp.where(live, st, 0.0)
+                s1 = ms if s1 is None else s1 + ms
+            total = (wt * r) * s1 if total is None else total + (wt * r) * s1
+        return total
 
     def first(a, i):
         L = own_x + i + a
@@ -208,9 +255,7 @@
                 sq = bx * bx + by * by + bz * bz
                 inv = lax.rsqrt(sq)
                 st = sq * inv - r
-                kp, km = NUMBER[(a, b, c)], NUMBER[(-a, b, c)]
-                word = kp // 16 + par * (km // 16 - kp // 16)
-                bit = (1 << (kp % 16)) + par * ((1 << (km % 16)) - (1 << (kp % 16)))
+                word, bit = where_bit(a, b, c)
                 live = (W[i, word] & bit) != 0
                 ms = jnp.where(live, st, 0.0)
                 hm = jnp.where(live, inv, 0.0)
@@ -262,8 +307,14 @@
                 block(a, i)
 
     inner(first)
-
-    q_load.wait()
+    for i in range(own_x):
+        SI[own_x + i] = ACC[0, i]
+
+    for c in q_loads:
+        c.wait()
+    bulk = moduli[0, material[0]]
+    shear = moduli[1, material[0]]
+    factor = 3.0 * bulk - 5.0 * shear
 
     def volumes(L, _):
         x = base + layer(L - own_x)
@@ -278,66 +329,92 @@
         shift_to(SB, L, 15.0 * shear / vol, 3)
         return 0
 
-    lax.fori_loop(0, 3 * own_x, volumes, 0)
-
-    for i in range(own_x):
-        L = 3 * own_x - 1 - i
-        to_partner(U, us, ur, i).wait_recv()
-
-        @pl.when(has_ahead)
-        def _():
-            to_ahead(U, fs, fr, i).start()
-
+    lax.fori_loop(0, own_x, volumes, 0)
+    for i in range(own_x):
+        to_partner(SI, ts, tr, i).start()
+    lax.fori_loop(own_x, 3 * own_x, volumes, 0)
+
+    def arrived(L):
         shift_u(L, 2)
         outer(first, L)
-    for i in range(own_x):
-        L = own_x - 1 - i
+        total = None
+        for i in range(own_x):
+            a = L - own_x - i
+            if -3 <= a <= 3:
+                part = across(a, i)
+                total = part if total is None else total + part
+        CX[L] = total
+
+    for i in range(own_x):
+        to_partner(U, us, ur, i).wait_recv()
+
+        @pl.when(has_ahead)
+        def _():
+            to_ahead(U, fs, fr, i).start()
+
+        arrived(3 * own_x - 1 - i)
+
+    n = own_x
+    part_up = remote(CX.at[pl.ds(2 * n, n)], RX.at[pl.ds(0, n)], xs.at[0], xr.at[0], ahead)
+    part_down = remote(CX.at[pl.ds(0, n)], RX.at[pl.ds(2 * n, n)], xs.at[1], xr.at[1], behind)
+
+    @pl.when(has_ahead)
+    def _():
+        part_up.start()
+
+    for i in range(own_x):
 
         @pl.when(has_behind)
         def _():
             to_ahead(U, fs, fr, i).wait_recv()
 
-        shift_u(L, 2)
-        outer(first, L)
-
-    factor = 3.0 * bulk - 5.0 * shear
+        arrived(own_x - 1 - i)
 
     def dilate(i, _):
         vol = V[own_x + i]
-        AL[own_x + i] = factor * (3.0 * ACC[0, i] / vol) / vol
+        a = factor * (3.0 * ACC[0, i] / vol) / vol
+        AL[own_x + i] = a
+        shift_to(SA, own_x + i, a, 3)
         return 0
 
     lax.fori_loop(0, own_x, dilate, 0)
 
-    def shift_a(i, _):
-        shift_to(SA, own_x + i, AL[own_x + i], 3)
-        return 0
-
-    lax.fori_loop(0, own_x, shift_a, 0)
-    for i in range(own_x):
-        to_partner(AL, ts, tr, i).start()
+    @pl.when(has_behind)
+    def _():
+        part_down.start()
+
+    for i in range(own_x):
+        to_partner(SI, ts, tr, i).wait_recv()
+
+        @pl.when(has_ahead)
+        def _():
+            to_ahead(SI, gs, gr, i).start()
 
     inner(second)
 
-    for i in range(own_x):
-        L = 3 * own_x - 1 - i
-        to_partner(AL, ts, tr, i).wait_recv()
-
-        @pl.when(has_ahead)
-        def _():
-            to_ahead(AL, gs, gr, i).start()
-
-        shift_to(SA, L, AL[L], 2)
+    def halo(L):
+        vol = V[L]
+        shift_to(SA, L, factor * (3.0 * (SI[L] + CX[L] + RX[L]) / vol) / vol, 2)
         outer(second, L)
-    for i in range(own_x):
-        L = own_x - 1 - i
+
+    @pl.when(has_ahead)
+    def _():
+        part_down.wait_recv()
+
+    for i in range(own_x):
+        halo(3 * own_x - 1 - i)
+
+    @pl.when(has_behind)
+    def _():
+        part_up.wait_recv()
+
+    for i in range(own_x):
 
         @pl.when(has_behind)
         def _():
-            to_ahead(AL, gs, gr, i).wait_recv()
-
-        shift_to(SA, L, AL[L], 2)
-        outer(second, L)
+            to_ahead(SI, gs, gr, i).wait_recv()
+
+        halo(own_x - 1 - i)
 
     for c in v_loads:
         c.wait()
@@ -346,53 +423,56 @@
         kinetic = None
         for n in range(3):
             force = FA[n, i] * sign if n == 0 else FA[n, i]
+            FO[i, n] = force
             nv = VEL[i, n] + DT * force
-            OV[i, n] = nv
-            OU[i, n] = U[own_x + i, n] + DT * nv
             kinetic = nv * nv if kinetic is None else kinetic + nv * nv
         vol = V[own_x + i]
         th = 3.0 * ACC[0, i] / vol
         th2 = th * th
         strain = ACC[1, i] - (2.0 / 9.0) * th2 * vol + th2 * ACC[2, i] * (1.0 / 9.0)
         heat = heat + 0.5 * kinetic + 0.5 * bulk * th2 + 7.5 * shear * strain / vol
-    EB[px] = jnp.sum(heat, axis=0, keepdims=True)
+    EB[slab] = jnp.sum(heat, axis=0, keepdims=True)
 
     outs = []
     for i in range(own_x):
-        for src, dst in ((OV, nv_hbm), (OU, nu_hbm)):
-            c = pltpu.make_async_copy(src.at[i], dst.at[:, layer(i)], out_sem.at[len(outs)])
-            c.start()
-            outs.append(c)
-
-    rows = [remote(EB.at[px], EB.at[px], es.at[d], er.at[px], at_x(d)) for d in range(1, nxs)]
-    for c in rows:
+        c = pltpu.make_async_copy(FO.at[i], force_hbm.at[:, layer(i)], out_sem.at[i])
         c.start()
-    for d in range(1, nxs):
-        q = (px + d) % nxs
-        remote(EB.at[q], EB.at[q], es.at[d], er.at[q], at_x(d)).wait_recv()
-    group = EB[0]
-    for n in range(1, nxs):
-        group = group + EB[n]
-    EP[0] = group
-    last = remote(EP.at[0], EP.at[1], ps, pr, partner)
-    last.start()
+        outs.append(c)
+
+    peers = [(d, o) for o in (True, False) for d in range(nxs) if d or o]
+    rows = []
+    for n, (d, o) in enumerate(peers):
+        c = remote(EB.at[slab], EB.at[slab], es.at[n], er.at[slab], (ens, slab_at(d, o)))
+        c.start()
+        rows.append(c)
     for c in outs:
         c.wait()
     for i in range(own_x):
         to_partner(U, us, ur, i).wait_send()
-        to_partner(AL, ts, tr, i).wait_send()
+        to_partner(SI, ts, tr, i).wait_send()
 
         @pl.when(has_ahead)
         def _():
             to_ahead(U, fs, fr, i).wait_send()
-            to_ahead(AL, gs, gr, i).wait_send()
+            to_ahead(SI, gs, gr, i).wait_send()
+
+    @pl.when(has_ahead)
+    def _():
+        part_up.wait_send()
+
+    @pl.when(has_behind)
+    def _():
+        part_down.wait_send()
 
     for c in rows:
         c.wait_send()
-    last.wait_recv()
-    both = EP[0] + EP[1]
-    en_ref[...] = jnp.broadcast_to(jnp.sum(both, axis=1, keepdims=True), en_ref.shape) * (1.0 / (nx * ny * nz))
-    last.wait_send()
+    for n, (d, o) in enumerate(peers):
+        q = slab_at(d, o)
+        remote(EB.at[q], EB.at[q], es.at[n], er.at[q], (ens, q)).wait_recv()
+    whole = EB[0]
+    for n in range(1, sx):
+        whole = whole + EB[n]
+    en_ref[...] = jnp.broadcast_to(jnp.sum(whole, axis=1, keepdims=True), en_ref.shape) * (1.0 / (nx * ny * nz))
 
 
 def solution(mesh):
@@ -402,27 +482,29 @@
         own_x, ny, nz = displacement.shape[1:]
         words = bond_mask.shape[0]
         nx = own_x * slabs
-        in_x, in_yz, plane = tables(nx, ny, nz, words)
+        in_yz, plane = tables(ny, nz, words)
         grid = (ny, nz)
         tall = (ny + 16, nz)
         nb = len(OFFSETS)
         vm = pltpu.VMEM
         dma = pltpu.SemaphoreType.DMA
         hbm = pl.BlockSpec(memory_space=pl.ANY)
-        smem = pl.BlockSpec(memory_space=pltpu.SMEM)
-        full = jax.ShapeDtypeStruct(displacement.shape, F32)
-        nu, nv, en = pl.pallas_call(
+        force, en = pl.pallas_call(
             functools.partial(kernel, slabs, nx),
-            out_shape=(full, full, jax.ShapeDtypeStruct((1, nz), F32)),
-            in_specs=[hbm] * 5 + [smem] * 3,
-            out_specs=(hbm, hbm, pl.BlockSpec(memory_space=pltpu.VMEM)),
+            out_shape=(jax.ShapeDtypeStruct(displacement.shape, F32), jax.ShapeDtypeStruct((1, nz), F32)),
+            in_specs=[hbm] * 7,
+            out_specs=(hbm, pl.BlockSpec(memory_space=pltpu.VMEM)),
             scratch_shapes=[
                 vm((3 * own_x, 3) + grid, F32),
                 vm((7, 3 * own_x, 3) + tall, F32),
                 vm((7, own_x) + grid, F32),
                 vm((own_x, words) + grid, jnp.int32),
+                vm((5, own_x, words) + tall, jnp.int32),
                 vm((words,) + grid, jnp.int32),
                 vm((4,) + grid, F32),
+                vm((3 * own_x,) + grid, F32),
+                vm((3 * own_x,) + grid, F32),
+                vm((3 * own_x,) + grid, F32),
                 vm((3 * own_x,) + grid, F32),
                 vm((7, 3 * own_x) + tall, F32),
                 vm((7, 3 * own_x) + tall, F32),
@@ -433,22 +515,23 @@
                 vm((3, own_x) + grid, F32),
                 vm((own_x, 3) + grid, F32),
                 vm((own_x, 3) + grid, F32),
-                vm((own_x, 3) + grid, F32),
-                vm((slabs // 2, 1, nz), F32),
-                vm((2, 1, nz), F32),
-                dma((3 * own_x + 2,)),
-                dma((2 * own_x,)),
+                vm((slabs, 1, nz), F32),
+                pltpu.SMEM(moduli.shape[::-1], F32),
+                pltpu.SMEM(material.shape, jnp.int32),
+                dma((3 * own_x + 4,)),
+                dma((own_x,)),
                 dma((own_x,)), dma((own_x,)), dma((own_x,)), dma((own_x,)),
                 dma((own_x,)), dma((own_x,)), dma((own_x,)), dma((own_x,)),
-                dma((slabs // 2,)), dma((slabs // 2,)),
-                dma, dma,
+                dma((2,)), dma((2,)),
+                dma((slabs,)), dma((slabs,)),
             ],
             compiler_params=pltpu.CompilerParams(collective_id=0, has_side_effects=True),
         )(
             displacement, velocity, bond_mask, jnp.asarray(in_yz), jnp.asarray(plane),
-            moduli, material, jnp.asarray(in_x.reshape(-1)),
+            moduli.T, material,
         )
-        return nu, nv, en[0, :1]
+        new_velocity = velocity + DT * force
+        return displacement + DT * new_velocity, new_velocity, en[0, :1]
 
     in_specs = (
         P("ens", "slab", None, None),

time: 57.6 us -> 53.6 us (0.931)
  the two profiles are of different devices: /device:TPU:40 before, /device:TPU:48 now
where the time goes in v1:
time: 53.6 us; the launch traced here: 53.4 us
  Pallas kernels  48.7 us (91%)
  between operations  2.48 us (5%)
  other arithmetic  1.6 us (3%)
  local copies, waits for them, and re-layouts  0.67 us (1%)
    pallas_call x1, Pallas kernels, body(): pl.pallas_call(functools.partial(kernel, slabs, nx), out_shape=(jax.Shape...  48.7 us
    add x1, other arithmetic, body(): return (displacement + DT * new_velocity, new_velocity, en[0, :1])  1.6 us

profile of v1, /device:TPU:48, one launch (start us, length us, event | category | flops | bytes accessed | tf_op | source)
XLA Modules:
  0.0 53.4 jit_solution(14521968319311129860)
XLA Ops:
  1.3 0.0 copy-start
  1.3 0.0 copy-start.1
  1.3 48.7 %shard_map.94 = (f32[3,3,24,128]{3,2,1,0:T(8,128)}, f32[1,128]{1,0:T(1,128)}) custom-call(f32[3,3,24,128]{3,2,1,0:T(8,128)} %u_hbm.1, f32[3,3,24,128]{3,2,1,0:T(8,128)} %v_hbm.1, s32[8,3,24,128]{3,2,1,0:T(8,128)} %w_hbm.1, s32[8,24,128]{2,1,0:T(8,128)} %constant.6.clone.yz_hbm, f32[4,24,128]{2,1,0:T(8,128)} %constant.7.clone.plane_hbm, f32[2,16]{1,0:T(2,128)} %bitcast.3, ...), custom_call_target="tpu_custom_call" | custom-call | tf_op jit(solution)/shard_map/pallas_call | solution.py:492
  50.0 0.0 copy-done
  50.0 0.0 copy-done.1
  50.0 1.6 %multiply_add_fusion = (f32[3,3,24,128]{3,2,1,0:T(8,128)}, f32[3,3,24,128]{3,2,1,0:T(8,128)}) fusion(f32[3,3,24,128]{3,2,1,0:T(8,128)S(1)} %copy-done, f32[3,3,24,128]{3,2,1,0:T(8,128)S(1)} %copy-done.1, f32[3,3,24,128]{3,2,1,0:T(8,128)} %get-tuple-element.5), kind=kLoop, calls=%fused_computation | loop fusion | flops 110592 | bytes 552960 | tf_op jit(solution)/shard_map/add | solution.py:534
  51.6 0.0 copy-start.2
  51.6 0.7 %copy-done.2 = f32[1,128]{1,0:T(1,128)S(1)} copy-done((f32[1,128]{1,0:T(1,128)S(1)}, f32[1,128]{1,0:T(1,128)}, u32[]{:S(2)}) %copy-start.2) | copy-done | bytes 536
Async XLA Ops:
  1.3 48.7 %copy-start = (f32[3,3,24,128]{3,2,1,0:T(8,128)S(1)}, f32[3,3,24,128]{3,2,1,0:T(8,128)}, u32[]{:S(2)}) copy-start(f32[3,3,24,128]{3,2,1,0:T(8,128)} %u_hbm.1) | copy-start | bytes 331780
  1.3 48.7 %copy-start.1 = (f32[3,3,24,128]{3,2,1,0:T(8,128)S(1)}, f32[3,3,24,128]{3,2,1,0:T(8,128)}, u32[]{:S(2)}) copy-start(f32[3,3,24,128]{3,2,1,0:T(8,128)} %v_hbm.1) | copy-start | bytes 331780
  51.6 0.7 %copy-start.2 = (f32[1,128]{1,0:T(1,128)S(1)}, f32[1,128]{1,0:T(1,128)}, u32[]{:S(2)}) copy-start(f32[1,128]{1,0:T(1,128)} %get-tuple-element.6) | copy-start | bytes 1540

commit v2 on v1

--- a/solution.py
+++ b/solution.py
@@ -132,9 +132,16 @@
     for c in u_loads:
         c.wait()
     pl.semaphore_wait(barrier, nxs)
-    for i in range(own_x):
-        to_partner(U, us, ur, i).start()
-
+    rank = (ens // 2) % 8
+    turn = jnp.where(rank > 4, 1 + rank % 2, 0)
+
+    def send_u(now):
+        @pl.when(turn == now)
+        def _():
+            for i in range(own_x):
+                to_partner(U, us, ur, i).start()
+
+    send_u(0)
     sign = step.astype(F32)
     zero = jnp.zeros((8, nz), F32)
 
@@ -306,7 +313,9 @@
             if -3 <= a <= 3:
                 block(a, i)
 
+    send_u(1)
     inner(first)
+    send_u(2)
     for i in range(own_x):
         SI[own_x + i] = ACC[0, i]
 
@@ -472,7 +481,14 @@
     whole = EB[0]
     for n in range(1, sx):
         whole = whole + EB[n]
-    en_ref[...] = jnp.broadcast_to(jnp.sum(whole, axis=1, keepdims=True), en_ref.shape) * (1.0 / (nx * ny * nz))
+    en_ref[...] = whole
+
+
+def finish(cells, force, heat, displacement, velocity, nu, nv, energy):
+    moved = velocity[...] + DT * force[...]
+    nv[...] = moved
+    nu[...] = displacement[...] + DT * moved
+    energy[0] = jnp.sum(heat[...]) * (1.0 / cells)
 
 
 def solution(mesh):
@@ -488,12 +504,13 @@
         nb = len(OFFSETS)
         vm = pltpu.VMEM
         dma = pltpu.SemaphoreType.DMA
-        hbm = pl.BlockSpec(memory_space=pl.ANY)
+        hbm = pl.BlockSpec(memory_space=pltpu.HBM)
+        vmem = pl.BlockSpec(memory_space=pltpu.VMEM)
         force, en = pl.pallas_call(
             functools.partial(kernel, slabs, nx),
             out_shape=(jax.ShapeDtypeStruct(displacement.shape, F32), jax.ShapeDtypeStruct((1, nz), F32)),
             in_specs=[hbm] * 7,
-            out_specs=(hbm, pl.BlockSpec(memory_space=pltpu.VMEM)),
+            out_specs=(hbm, vmem),
             scratch_shapes=[
                 vm((3 * own_x, 3) + grid, F32),
                 vm((7, 3 * own_x, 3) + tall, F32),
@@ -530,8 +547,13 @@
             displacement, velocity, bond_mask, jnp.asarray(in_yz), jnp.asarray(plane),
             moduli.T, material,
         )
-        new_velocity = velocity + DT * force
-        return displacement + DT * new_velocity, new_velocity, en[0, :1]
+        full = jax.ShapeDtypeStruct(displacement.shape, F32)
+        return pl.pallas_call(
+            functools.partial(finish, nx * ny * nz),
+            out_shape=(full, full, jax.ShapeDtypeStruct((1,), F32)),
+            in_specs=[vmem] * 4,
+            out_specs=(vmem, vmem, pl.BlockSpec(memory_space=pltpu.SMEM)),
+        )(force, en, displacement, velocity)
 
     in_specs = (
         P("ens", "slab", None, None),

time: 53.6 us -> 48 us (0.90)
  the two profiles are of different devices: /device:TPU:48 before, /device:TPU:200 now
where the time goes in v2:
time: 48 us; the launch traced here: 47.8 us
  Pallas kernels  46.5 us (97%)
  between operations  1.29 us (3%)
    pallas_call x1, Pallas kernels, body(): pl.pallas_call(functools.partial(kernel, slabs, nx), out_shape=(jax.Shape...  44.8 us
    pallas_call x1, Pallas kernels, body(): pl.pallas_call(functools.partial(finish, nx * ny * nz), out_shape=(full,...  1.72 us

profile of v2, /device:TPU:200, one launch (start us, length us, event | category | flops | bytes accessed | tf_op | source)
XLA Modules:
  0.0 47.8 jit_solution(4317092879655236230)
XLA Ops:
  1.3 44.8 %shard_map.94 = (f32[3,3,24,128]{3,2,1,0:T(8,128)}, f32[1,128]{1,0:T(1,128)}) custom-call(f32[3,3,24,128]{3,2,1,0:T(8,128)} %displacement.1, f32[3,3,24,128]{3,2,1,0:T(8,128)} %velocity.1, s32[8,3,24,128]{3,2,1,0:T(8,128)} %w_hbm.1, s32[8,24,128]{2,1,0:T(8,128)} %constant.4.clone.yz_hbm, f32[4,24,128]{2,1,0:T(8,128)} %constant.5.clone.plane_hbm, ...), custom_call_target="tpu_custom_call" | custom-call | tf_op jit(solution)/shard_map/pallas_call | solution.py:509
  46.1 1.7 %shard_map.95 = (f32[3,3,24,128]{3,2,1,0:T(8,128)}, f32[3,3,24,128]{3,2,1,0:T(8,128)}, f32[1]{0:T(128)}) custom-call(f32[3,3,24,128]{3,2,1,0:T(8,128)} %get-tuple-element.5.force, f32[1,128]{1,0:T(1,128)} %get-tuple-element.6.heat, f32[3,3,24,128]{3,2,1,0:T(8,128)} %displacement.1, f32[3,3,24,128]{3,2,1,0:T(8,128)} %velocity.1), custom_call_target="tpu_custom_call" | custom-call | tf_op jit(solution)/shard_map/pallas_call | solution.py:551

commit v3 on v2

--- a/solution.py
+++ b/solution.py
@@ -106,7 +106,7 @@
     w_loads = [load(w_hbm.at[:, layer(i)], W.at[i]) for i in range(own_x)]
     w_loads.append(load(yz_hbm, YZ))
     q_loads = [load(plane_hbm, Q), load(moduli_hbm, moduli), load(material_hbm, material)]
-    v_loads = [load(v_hbm.at[:, layer(i)], VEL.at[i]) for i in range(own_x)]
+    v_load = load(v_hbm, VEL)
 
     def remote(src, dst, send, recv, dev):
         return pltpu.make_async_remote_copy(
@@ -133,7 +133,7 @@
         c.wait()
     pl.semaphore_wait(barrier, nxs)
     rank = (ens // 2) % 8
-    turn = jnp.where(rank > 4, 1 + rank % 2, 0)
+    turn = jnp.where(rank > 4, 1 + rank // 7, 0)
 
     def send_u(now):
         @pl.when(turn == now)
@@ -317,7 +317,7 @@
     inner(first)
     send_u(2)
     for i in range(own_x):
-        SI[own_x + i] = ACC[0, i]
+        SI[2 * own_x - 1 - i] = ACC[0, i]
 
     for c in q_loads:
         c.wait()
@@ -339,8 +339,10 @@
         return 0
 
     lax.fori_loop(0, own_x, volumes, 0)
-    for i in range(own_x):
-        to_partner(SI, ts, tr, i).start()
+    n = own_x
+    sums_over = remote(SI.at[pl.ds(n, n)], SI.at[pl.ds(2 * n, n)], ts, tr, partner)
+    sums_on = remote(SI.at[pl.ds(2 * n, n)], SI.at[pl.ds(0, n)], gs, gr, ahead)
+    sums_over.start()
     lax.fori_loop(own_x, 3 * own_x, volumes, 0)
 
     def arrived(L):
@@ -363,7 +365,6 @@
 
         arrived(3 * own_x - 1 - i)
 
-    n = own_x
     part_up = remote(CX.at[pl.ds(2 * n, n)], RX.at[pl.ds(0, n)], xs.at[0], xr.at[0], ahead)
     part_down = remote(CX.at[pl.ds(0, n)], RX.at[pl.ds(2 * n, n)], xs.at[1], xr.at[1], behind)
 
@@ -392,12 +393,11 @@
     def _():
         part_down.start()
 
-    for i in range(own_x):
-        to_partner(SI, ts, tr, i).wait_recv()
-
-        @pl.when(has_ahead)
-        def _():
-            to_ahead(SI, gs, gr, i).start()
+    sums_over.wait_recv()
+
+    @pl.when(has_ahead)
+    def _():
+        sums_on.start()
 
     inner(second)
 
@@ -417,23 +417,21 @@
     def _():
         part_up.wait_recv()
 
-    for i in range(own_x):
-
-        @pl.when(has_behind)
-        def _():
-            to_ahead(SI, gs, gr, i).wait_recv()
-
+    @pl.when(has_behind)
+    def _():
+        sums_on.wait_recv()
+
+    for i in range(own_x):
         halo(own_x - 1 - i)
 
-    for c in v_loads:
-        c.wait()
+    v_load.wait()
     heat = jnp.zeros((ny, nz), F32)
     for i in range(own_x):
         kinetic = None
         for n in range(3):
             force = FA[n, i] * sign if n == 0 else FA[n, i]
-            FO[i, n] = force
-            nv = VEL[i, n] + DT * force
+            FO[n, layer(i)] = force
+            nv = VEL[n, layer(i)] + DT * force
             kinetic = nv * nv if kinetic is None else kinetic + nv * nv
         vol = V[own_x + i]
         th = 3.0 * ACC[0, i] / vol
@@ -442,11 +440,8 @@
         heat = heat + 0.5 * kinetic + 0.5 * bulk * th2 + 7.5 * shear * strain / vol
     EB[slab] = jnp.sum(heat, axis=0, keepdims=True)
 
-    outs = []
-    for i in range(own_x):
-        c = pltpu.make_async_copy(FO.at[i], force_hbm.at[:, layer(i)], out_sem.at[i])
-        c.start()
-        outs.append(c)
+    out = pltpu.make_async_copy(FO, force_hbm, out_sem)
+    out.start()
 
     peers = [(d, o) for o in (True, False) for d in range(nxs) if d or o]
     rows = []
@@ -454,20 +449,20 @@
         c = remote(EB.at[slab], EB.at[slab], es.at[n], er.at[slab], (ens, slab_at(d, o)))
         c.start()
         rows.append(c)
-    for c in outs:
-        c.wait()
+    out.wait()
     for i in range(own_x):
         to_partner(U, us, ur, i).wait_send()
-        to_partner(SI, ts, tr, i).wait_send()
 
         @pl.when(has_ahead)
         def _():
             to_ahead(U, fs, fr, i).wait_send()
-            to_ahead(SI, gs, gr, i).wait_send()
+
+    sums_over.wait_send()
 
     @pl.when(has_ahead)
     def _():
         part_up.wait_send()
+        sums_on.wait_send()
 
     @pl.when(has_behind)
     def _():
@@ -530,15 +525,15 @@
                 vm((nb, own_x) + grid, F32),
                 vm((nb, own_x) + grid, F32),
                 vm((3, own_x) + grid, F32),
-                vm((own_x, 3) + grid, F32),
-                vm((own_x, 3) + grid, F32),
+                vm((3, own_x) + grid, F32),
+                vm((3, own_x) + grid, F32),
                 vm((slabs, 1, nz), F32),
                 pltpu.SMEM(moduli.shape[::-1], F32),
                 pltpu.SMEM(material.shape, jnp.int32),
-                dma((3 * own_x + 4,)),
-                dma((own_x,)),
+                dma((2 * own_x + 5,)),
+                dma,
                 dma((own_x,)), dma((own_x,)), dma((own_x,)), dma((own_x,)),
-                dma((own_x,)), dma((own_x,)), dma((own_x,)), dma((own_x,)),
+                dma, dma, dma, dma,
                 dma((2,)), dma((2,)),
                 dma((slabs,)), dma((slabs,)),
             ],

time: 48 us -> 47.7 us (level)
  the two profiles are of different devices: /device:TPU:200 before, /device:TPU:208 now
where the time goes in v3:
time: 47.7 us; the launch traced here: 47.5 us
  Pallas kernels  46.3 us (97%)
  between operations  1.29 us (3%)
    pallas_call x1, Pallas kernels, body(): pl.pallas_call(functools.partial(kernel, slabs, nx), out_shape=(jax.Shape...  44.5 us
    pallas_call x1, Pallas kernels, body(): pl.pallas_call(functools.partial(finish, nx * ny * nz), out_shape=(full,...  1.72 us

profile of v3, /device:TPU:208, one launch (start us, length us, event | category | flops | bytes accessed | tf_op | source)
XLA Modules:
  0.0 47.5 jit_solution(15402503698010454512)
XLA Ops:
  1.3 44.5 %shard_map.94 = (f32[3,3,24,128]{3,2,1,0:T(8,128)}, f32[1,128]{1,0:T(1,128)}) custom-call(f32[3,3,24,128]{3,2,1,0:T(8,128)} %displacement.1, f32[3,3,24,128]{3,2,1,0:T(8,128)} %velocity.1, s32[8,3,24,128]{3,2,1,0:T(8,128)} %w_hbm.1, s32[8,24,128]{2,1,0:T(8,128)} %constant.4.clone.yz_hbm, f32[4,24,128]{2,1,0:T(8,128)} %constant.5.clone.plane_hbm, ...), custom_call_target="tpu_custom_call" | custom-call | tf_op jit(solution)/shard_map/pallas_call | solution.py:504
  45.8 1.7 %shard_map.95 = (f32[3,3,24,128]{3,2,1,0:T(8,128)}, f32[3,3,24,128]{3,2,1,0:T(8,128)}, f32[1]{0:T(128)}) custom-call(f32[3,3,24,128]{3,2,1,0:T(8,128)} %get-tuple-element.5.force, f32[1,128]{1,0:T(1,128)} %get-tuple-element.6.heat, f32[3,3,24,128]{3,2,1,0:T(8,128)} %displacement.1, f32[3,3,24,128]{3,2,1,0:T(8,128)} %velocity.1), custom_call_target="tpu_custom_call" | custom-call | tf_op jit(solution)/shard_map/pallas_call | solution.py:546
